TPU v7x, 32 devices: a whole 2x2x4 slice. The times are simulated.
32 devices in a mesh: gx: 8 (over z, y), gy: 4 (over x, core).
Axes of the slice: x: 2, y: 2, z: 4, core: 2. Of those that a mesh axis runs over, the one named last changes fastest.
Arguments:
- charge_density: float32 [256, 256, 256], P('gx', 'gy'), may hold values from -5080 to 5140
Outputs:
- potential: float32 [256, 256, 256], P('gx', 'gy')
- energies: float32 [2], replicated
All inputs are finite; a program needn't handle non-finite values.
Results may differ from a plain program's by a relative error of at most 0.0003.
Values sent between devices are 32-bit elements.
A program may use at most 192 MiB of HBM per device.

v0:
```python
import math
import jax
import jax.numpy as jnp
import numpy as np
from jax import lax
from jax.sharding import PartitionSpec as P

ORDER = 16
exact_mode = lax.Precision.HIGHEST
outer_ratio = 1.1
radius_scale = math.sqrt(3.0) / 2.0


def sine_table(length):
    counter = jnp.arange(length, dtype=jnp.int32) + 1
    product = counter[:, None] * counter[None, :] % (2 * (length + 1))
    return jnp.sin(math.pi * product.astype(jnp.float32) / (length + 1))


def eigen_line(counter, length):
    half_angle = math.pi * (counter + 1).astype(jnp.float32) / (2.0 * (length + 1))
    return 4.0 * float((length + 1) * (length + 1)) * jnp.sin(half_angle) ** 2


def recurrence_tables():
    degree_count = ORDER + 1
    near_coeff = np.zeros((degree_count, degree_count, 1), np.float32)
    far_coeff = np.zeros((degree_count, degree_count, 1), np.float32)
    sector = np.ones(degree_count, np.float32)
    for degree in range(1, degree_count):
        for azimuth in range(degree):
            divisor = math.sqrt(degree * degree - azimuth * azimuth)
            near_coeff[degree, azimuth, 0] = (2 * degree - 1) / divisor
            far_coeff[degree, azimuth, 0] = (
                math.sqrt((degree - 1) * (degree - 1) - azimuth * azimuth) / divisor
            )
        if degree >= 2:
            sector[degree] = math.sqrt((2 * degree - 1) / (2.0 * degree))
    return (near_coeff, far_coeff, sector)


def expansion_weights():
    degree_count = ORDER + 1
    weights = np.zeros((degree_count, degree_count), np.float32)
    for degree in range(degree_count):
        for azimuth in range(degree + 1):
            factor = 1.0 if azimuth == 0 else 2.0
            weights[degree, azimuth] = factor / (
                4.0 * math.pi * radius_scale * outer_ratio ** (degree + 1)
            )
    return weights


def harmonic_sweep(unit_x, unit_y, unit_z, visitor, running):
    near_coeff, far_coeff, sector = recurrence_tables()
    degree_count = ORDER + 1
    selector = np.eye(degree_count, dtype=np.float32)[:, :, None]
    empty_rows = jnp.zeros((degree_count,) + unit_x.shape, unit_x.dtype)
    sector_cosine = jnp.ones_like(unit_x)
    sector_sine = jnp.zeros_like(unit_x)
    cosine_prev, sine_prev, cosine_old, sine_old = (empty_rows, empty_rows, empty_rows, empty_rows)
    for degree in range(degree_count):
        if degree > 0:
            sector_cosine, sector_sine = (
                sector[degree] * (unit_x * sector_cosine - unit_y * sector_sine),
                sector[degree] * (unit_x * sector_sine + unit_y * sector_cosine),
            )
        cosine_now = (
            near_coeff[degree] * unit_z * cosine_prev
            - far_coeff[degree] * cosine_old
            + selector[degree] * sector_cosine
        )
        sine_now = (
            near_coeff[degree] * unit_z * sine_prev
            - far_coeff[degree] * sine_old
            + selector[degree] * sector_sine
        )
        running = visitor(running, degree, cosine_now, sine_now)
        cosine_old, sine_old = (cosine_prev, sine_prev)
        cosine_prev, sine_prev = (cosine_now, sine_now)
    return running


def face_moments(point_x, point_y, point_z, charge):
    radius = jnp.sqrt(point_x * point_x + point_y * point_y + point_z * point_z)
    scaled_radius = radius / radius_scale

    def visitor(running, degree, cosine_now, sine_now):
        weight, moment_cosine, moment_sine, facing_cosine, facing_sine = running
        moment_cosine = moment_cosine + [jnp.dot(cosine_now, weight, precision=exact_mode)]
        moment_sine = moment_sine + [jnp.dot(sine_now, weight, precision=exact_mode)]
        facing_cosine = facing_cosine + [jnp.dot(cosine_now, charge, precision=exact_mode)]
        facing_sine = facing_sine + [jnp.dot(sine_now, charge, precision=exact_mode)]
        return (weight * scaled_radius, moment_cosine, moment_sine, facing_cosine, facing_sine)

    result = harmonic_sweep(
        point_x / radius, point_y / radius, point_z / radius, visitor, (charge, [], [], [], [])
    )
    return tuple((jnp.stack(listing) for listing in result[1:]))


def face_potential(point_x, point_y, point_z, weight_cosine, weight_sine):
    radius = jnp.sqrt(point_x * point_x + point_y * point_y + point_z * point_z)

    def visitor(accum, degree, cosine_now, sine_now):
        accum = accum + jnp.dot(weight_cosine[degree], cosine_now, precision=exact_mode)
        return accum + jnp.dot(weight_sine[degree], sine_now, precision=exact_mode)

    return harmonic_sweep(
        point_x / radius, point_y / radius, point_z / radius, visitor, jnp.zeros_like(point_x)
    )


def moments_of(points):
    return face_moments(points[0], points[1], points[2], points[3])


def no_moments(points):
    empty_rows = jnp.zeros((ORDER + 1, ORDER + 1), jnp.float32)
    return (empty_rows, empty_rows, empty_rows, empty_rows)


def potential_of(points):
    return face_potential(points[0], points[1], points[2], points[3], points[4])


def no_potential(points):
    return jnp.zeros_like(points[0])


def forward(volume, sine_rows, swap_one, swap_two):
    cells_a, cells_b, length = volume.shape
    spectrum = jnp.einsum("abz,zk->kab", volume, sine_rows, precision=exact_mode)
    spectrum = swap_one(spectrum.reshape(length, cells_a * cells_b))
    groups_one = spectrum.shape[1] // (cells_a * cells_b)
    pieces = spectrum.reshape(spectrum.shape[0], groups_one, cells_a, cells_b)
    table_one = sine_rows.reshape(groups_one, cells_b, length)
    spectrum = jnp.einsum("zpab,pbj->jza", pieces, table_one, precision=exact_mode)
    depth_cells = spectrum.shape[1]
    spectrum = swap_two(spectrum.reshape(length, depth_cells * cells_a))
    groups_two = spectrum.shape[1] // (depth_cells * cells_a)
    pieces = spectrum.reshape(spectrum.shape[0], groups_two, depth_cells, cells_a)
    table_two = sine_rows.reshape(groups_two, cells_a, length)
    return jnp.einsum("kqzc,qcj->kzj", pieces, table_two, precision=exact_mode)


def inverse(spectrum, sine_rows, back_two, back_one, cells_a, cells_b):
    rows_one, depth_cells, length = spectrum.shape
    groups_two = length // cells_a
    groups_one = length // cells_b
    table_two = sine_rows.reshape(length, groups_two, cells_a)
    pieces = jnp.einsum("kzj,jqc->kqzc", spectrum, table_two, precision=exact_mode)
    pieces = back_two(pieces.reshape(rows_one, groups_two * depth_cells * cells_a))
    pieces = pieces.reshape(length, depth_cells, cells_a)
    table_one = sine_rows.reshape(length, groups_one, cells_b)
    volume = jnp.einsum("jza,jpb->zpab", pieces, table_one, precision=exact_mode)
    volume = back_one(volume.reshape(depth_cells, groups_one * cells_a * cells_b))
    volume = volume.reshape(length, cells_a, cells_b)
    return jnp.einsum("kab,kz->abz", volume, sine_rows, precision=exact_mode)


def shards(charge_density):
    cells_a, cells_b, length = charge_density.shape
    spacing = 1.0 / (length + 1)
    sine_rows = sine_table(length)
    index_x = lax.axis_index("gx")
    index_y = lax.axis_index("gy")

    def swap_one(operand):
        return lax.all_to_all(operand, "gy", split_axis=0, concat_axis=1, tiled=True)

    def swap_two(operand):
        return lax.all_to_all(operand, "gx", split_axis=0, concat_axis=1, tiled=True)

    def back_two(operand):
        return lax.all_to_all(operand, "gx", split_axis=1, concat_axis=0, tiled=True)

    def back_one(operand):
        return lax.all_to_all(operand, "gy", split_axis=1, concat_axis=0, tiled=True)

    groups_one = lax.axis_size("gy")
    groups_two = lax.axis_size("gx")
    count_one = length // groups_two
    count_two = length // groups_one
    eigen_one = eigen_line(index_x * count_one + jnp.arange(count_one, dtype=jnp.int32), length)
    eigen_two = eigen_line(index_y * count_two + jnp.arange(count_two, dtype=jnp.int32), length)
    eigen_full = eigen_line(jnp.arange(length, dtype=jnp.int32), length)
    denominator = (
        eigen_one[:, None, None] + eigen_two[None, :, None] + eigen_full[None, None, :]
    ) * ((length + 1) / 2.0) ** 3

    def back_of(spectrum):
        return inverse(spectrum, sine_rows, back_two, back_one, cells_a, cells_b)

    charge_spectrum = forward(charge_density, sine_rows, swap_one, swap_two) / denominator
    first_field = back_of(charge_spectrum)
    energy_first = spacing**3 * jnp.sum(charge_density * first_field)
    coords_x = (
        (index_x * cells_a + jnp.arange(cells_a, dtype=jnp.int32)).astype(jnp.float32)
        - (length - 1) / 2.0
    ) * spacing
    coords_y = (
        (index_y * cells_b + jnp.arange(cells_b, dtype=jnp.int32)).astype(jnp.float32)
        - (length - 1) / 2.0
    ) * spacing
    coords_z = (jnp.arange(length, dtype=jnp.float32) - (length - 1) / 2.0) * spacing
    face_x = jnp.broadcast_to(coords_x[:, None], (cells_a, cells_b)).reshape(-1)
    face_y = jnp.broadcast_to(coords_y[None, :], (cells_a, cells_b)).reshape(-1)
    plane_z = jnp.full((cells_a * cells_b,), 0.5, jnp.float32)
    side_y = jnp.broadcast_to(coords_y[:, None], (cells_b, length)).reshape(-1)
    side_depth_b = jnp.broadcast_to(coords_z[None, :], (cells_b, length)).reshape(-1)
    plane_b = jnp.full((cells_b * length,), 0.5, jnp.float32)
    side_x = jnp.broadcast_to(coords_x[:, None], (cells_a, length)).reshape(-1)
    side_depth_a = jnp.broadcast_to(coords_z[None, :], (cells_a, length)).reshape(-1)
    plane_a = jnp.full((cells_a * length,), 0.5, jnp.float32)
    boundary_faces = [
        (face_x, face_y, -plane_z, first_field[:, :, 0], None),
        (face_x, face_y, plane_z, first_field[:, :, -1], None),
        (-plane_b, side_y, side_depth_b, first_field[0], index_x == 0),
        (plane_b, side_y, side_depth_b, first_field[-1], index_x == lax.axis_size("gx") - 1),
        (side_x, -plane_a, side_depth_a, first_field[:, 0], index_y == 0),
        (side_x, plane_a, side_depth_a, first_field[:, -1], index_y == lax.axis_size("gy") - 1),
    ]
    totals = None
    for point_x, point_y, point_z, near_cells, owning in boundary_faces:
        points = (point_x, point_y, point_z, spacing * near_cells.reshape(-1))
        if owning is None:
            face_terms = moments_of(points)
        else:
            face_terms = lax.cond(owning, moments_of, no_moments, points)
        if totals is None:
            totals = face_terms
        else:
            totals = tuple((earlier + later for earlier, later in zip(totals, face_terms)))
    mom_cosine, mom_sine, dir_cosine, dir_sine = totals
    sum_cosine, sum_sine = lax.psum((mom_cosine, mom_sine), ("gx", "gy"))
    weights = expansion_weights()
    weight_cosine = weights * sum_cosine
    weight_sine = weights * sum_sine
    potentials = []
    for point_x, point_y, point_z, near_cells, owning in boundary_faces:
        points = (point_x, point_y, point_z, weight_cosine, weight_sine)
        if owning is None:
            potentials.append(potential_of(points) / spacing**2)
        else:
            potentials.append(lax.cond(owning, potential_of, no_potential, points) / spacing**2)
    planes = jnp.stack(
        [potentials[0].reshape(cells_a, cells_b), potentials[1].reshape(cells_a, cells_b)]
    )
    lead_walls = jnp.stack(
        [potentials[4].reshape(cells_a, length), potentials[5].reshape(cells_a, length)]
    )
    tail_walls = jnp.stack(
        [potentials[2].reshape(cells_b, length), potentials[3].reshape(cells_b, length)]
    )
    plane_width = 2 * cells_a * cells_b // count_two
    plane_part = jnp.broadcast_to(
        planes.reshape(1, count_two, plane_width), (groups_one, count_two, plane_width)
    ).reshape(length, plane_width)
    lead_depth = jnp.einsum("ftz,zk->kft", lead_walls, sine_rows, precision=exact_mode).reshape(
        length, 2 * cells_a
    )
    tail_depth = jnp.einsum("fbz,zk->kfb", tail_walls, sine_rows, precision=exact_mode).reshape(
        length, 2 * cells_b
    )
    received = swap_one(jnp.concatenate([plane_part, lead_depth, tail_depth], axis=1))
    received = received.reshape(count_two, groups_one, -1)
    plane_all = jnp.transpose(received[:, :, :plane_width], (1, 0, 2)).reshape(
        groups_one, 2, cells_a, cells_b
    )
    lead_total = jnp.sum(
        received[:, :, plane_width : plane_width + 2 * cells_a].reshape(
            count_two, groups_one, 2, cells_a
        ),
        axis=1,
    )
    tail_part = received[:, :, plane_width + 2 * cells_a :].reshape(
        count_two, groups_one, 2, cells_b
    )
    lead_table = sine_rows.reshape(groups_one, cells_b, length)
    plane_lead = jnp.einsum("pftb,pbj->jft", plane_all, lead_table, precision=exact_mode).reshape(
        length, 2 * cells_a
    )
    tail_lead = jnp.einsum("kpfb,pbj->jfk", tail_part, lead_table, precision=exact_mode).reshape(
        length, 2 * count_two
    )
    lead_width = 2 * count_two * cells_a // count_one
    lead_copies = jnp.broadcast_to(
        lead_total.reshape(1, count_one, lead_width), (groups_two, count_one, lead_width)
    ).reshape(length, lead_width)
    received = swap_two(jnp.concatenate([plane_lead, lead_copies, tail_lead], axis=1))
    received = received.reshape(count_one, groups_two, -1)
    tail_table = sine_rows.reshape(groups_two, cells_a, length)
    plane_modes = jnp.einsum(
        "jqft,qtm->jfm",
        received[:, :, : 2 * cells_a].reshape(count_one, groups_two, 2, cells_a),
        tail_table,
        precision=exact_mode,
    )
    lead_all = jnp.transpose(
        received[:, :, 2 * cells_a : 2 * cells_a + lead_width], (1, 0, 2)
    ).reshape(groups_two, count_two, 2, cells_a)
    lead_modes = jnp.einsum("qkft,qtm->fkm", lead_all, tail_table, precision=exact_mode)
    tail_modes = jnp.sum(
        received[:, :, 2 * cells_a + lead_width :].reshape(count_one, groups_two, 2, count_two),
        axis=1,
    )
    edge_rows = jnp.stack([sine_rows[0], sine_rows[-1]])
    depth_edge = lax.dynamic_slice_in_dim(edge_rows, index_y * count_two, count_two, 1)
    mode_edge = lax.dynamic_slice_in_dim(edge_rows, index_x * count_one, count_one, 1)
    result = jnp.einsum("jfm,fk->jkm", plane_modes, depth_edge, precision=exact_mode)
    result = result + jnp.einsum("fj,fkm->jkm", mode_edge, lead_modes, precision=exact_mode)
    potential = back_of(
        charge_spectrum
        + (result + jnp.einsum("jfk,fm->jkm", tail_modes, edge_rows, precision=exact_mode))
        / denominator
    )
    first_energy, second_energy = lax.psum(
        (energy_first, spacing**3 * jnp.sum(charge_density * potential)), ("gx", "gy")
    )
    return (potential, jnp.stack([first_energy, second_energy]))


def solution(mesh):
    placed = (P("gx", "gy", None),)
    return jax.shard_map(
        shards, mesh=mesh, in_specs=placed, out_specs=(P("gx", "gy", None), P()), check_vma=False
    )
```

profile of v0, /device:TPU:0, one launch (start us, length us, event | category | flops | bytes accessed | tf_op | source)
XLA Modules:
  0.0 1063.5 jit_solution(1481408688920894633)
XLA Ops:
  0.6 4.5 fusion.1266
  8.2 4.7 copy.900
  13.0 4.2 all-to-all-start
  17.3 25.6 %all-to-all-done = f32[4,64,2048]{2,1,0:T(8,128)S(1)} async-done(((f32[4,64,2048]{2,1,0:T(8,128)}), f32[4,64,2048]{2,1,0:T(8,128)S(1)}, u32[]{:S(2)}, u32[]{:S(2)}) %all-to-all-start) | async-done | bytes 2097184 | tf_op jit(solution)/shard_map/all_to_all | solution.py:170
  45.9 9.2 convolution_bitcast_fusion
  55.1 6.9 all-to-all-start.1
  62.3 59.0 %all-to-all-done.1 = f32[8,32,2048]{2,1,0:T(8,128)S(1)} async-done(((f32[8,32,2048]{2,1,0:T(8,128)}), f32[8,32,2048]{2,1,0:T(8,128)S(1)}, u32[]{:S(2)}, u32[]{:S(2)}) %all-to-all-start.1) | async-done | bytes 2097184 | tf_op jit(solution)/shard_map/all_to_all | solution.py:173
  121.3 4.8 reshape.2046
  126.1 11.5 %bitcast_divide_fusion = f32[32,64,256]{2,1,0:T(8,128)S(1)} fusion(f32[32,8,64,32]{3,2,0,1:T(8,128)} %reshape.2046, f32[256]{0:T(256)S(1)} %multiply_multiply_fusion.64, f32[32,64]{1,0:T(8,128)S(1)} %broadcast_add_fusion, s32[256]{0:T(256)S(1)} %iota_add_fusion, s32[8,32]{1,0:T(8,128)S(1)} %add_add_fusion.7), kind=kOutput, calls=%fused_computation.1785 | convolution fusion | flops 1612775424 | bytes 4205568 | tf_op jit(solution)/shard_map/kqzc,qcj->kzj/dot_general | solution.py:144
  139.0 7.1 convolution_bitcast_fusion.2
  146.1 6.9 copy.905
  153.0 7.5 reshape.2047
  164.3 48.2 %all-to-all-done.2 = f32[32,8,2048]{2,0,1:T(8,128)S(1)} async-done(((f32[32,8,2048]{2,0,1:T(8,128)}), f32[32,8,2048]{2,0,1:T(8,128)S(1)}, u32[]{:S(2)}, u32[]{:S(2)}) %all-to-all-start.2) | async-done | bytes 2097184 | tf_op jit(solution)/shard_map/all_to_all | solution.py:176
  212.5 4.8 reshape.1197
  217.3 7.0 copy.872
  224.3 7.0 fusion.1211
  241.1 23.2 %all-to-all-done.3 = f32[64,4,2048]{2,0,1:T(8,128)S(1)} async-done(((f32[64,4,2048]{2,0,1:T(8,128)}), f32[64,4,2048]{2,0,1:T(8,128)S(1)}, u32[]{:S(2)}, u32[]{:S(2)}) %all-to-all-start.3) | async-done | bytes 2097184 | tf_op jit(solution)/shard_map/all_to_all | solution.py:179
  264.3 11.5 %reshape.1198 = f32[256,32,64]{2,1,0:T(8,128)} reshape(f32[4,64,2048]{2,1,0:T(8,128)S(1)} %bitcast.2772) | data formatting | bytes 4194304 | tf_op jit(solution)/shard_map/reshape | solution.py:158
  275.8 11.3 %fusion.1202 = f32[32,64,256]{2,1,0:T(8,128)S(1)} fusion(f32[256,32,64]{2,1,0:T(8,128)} %reshape.1198, s32[256]{0:T(256)S(1)} %iota_add_fusion), kind=kOutput, calls=%fused_computation.1780 | convolution fusion | flops 1611202560 | bytes 4195328 | tf_op jit(solution)/shard_map/kab,kz->abz/dot_general | solution.py:159
  373.3 10.0 conditional.9
  383.3 113.1 %conditional.8 = (f32[17,17]{1,0:T(8,128)S(1)}, f32[17,17]{1,0:T(8,128)S(1)}) conditional(s32[]{:T(128)} %convert_element_type.118, () %tuple.64, (f32[17,1]{0,1:T(1,128)S(1)}, f32[16384]{0:T(1024)}, f32[16384]{0:T(1024)S(1)}, f32[16384]{0:T(1024)S(1)}, f32[17,1]{0,1:T(1,128)S(1)}, /*index=5*/f32[17,1]{0,1:T(1,128)S(1)}, ...), branch_computations={%region_0.1_spmd, %region_1.2_spmd} | conditional | flops 290816064 | bytes 57925084 | solution.py:230
  391.5 4.6 fusion.115
  396.1 4.5 fusion.114
  400.6 4.3 fusion.113
  440.8 6.4 multiply_add_fusion.2
  472.0 7.8 multiply_add_fusion.17
  497.0 16.6 %conditional.11 = (f32[17,17]{1,0:T(8,128)S(1)}, f32[17,17]{1,0:T(8,128)S(1)}) conditional(s32[]{:T(128)} %convert_element_type.121, () %tuple.69, (f32[17,1]{0,1:T(1,128)S(1)}, f32[8192]{0:T(1024)S(1)}, f32[8192]{0:T(1024)S(1)}, f32[8192]{0:T(1024)S(1)}, f32[17,1]{0,1:T(1,128)S(1)}, /*index=5*/f32[17,1]{0,1:T(1,128)S(1)}, ...), branch_computations={%region_6.7_spmd, %region_7.8_spmd} | conditional | flops 145408080 | bytes 28004404 | solution.py:230
  514.2 54.3 %conditional.10 = (f32[17,17]{1,0:T(8,128)}, f32[17,17]{1,0:T(8,128)}) conditional(s32[]{:T(128)} %convert_element_type.120, () %tuple.67, (f32[17,1]{0,1:T(1,128)S(1)}, f32[8192]{0:T(1024)S(1)}, f32[8192]{0:T(1024)S(1)}, f32[8192]{0:T(1024)S(1)}, f32[17,1]{0,1:T(1,128)S(1)}, /*index=5*/f32[17,1]{0,1:T(1,128)S(1)}, f32[32,64,256]{2,1,0:T(8,128)S(1)}, ...), branch_computations={%region_4.5_spmd, %region_5.6_spmd} | conditional | flops 145408080 | bytes 27208952 | solution.py:230
  577.8 40.4 %all-reduce.1 = (f32[17,17]{1,0:T(8,128)S(1)}, f32[17,17]{1,0:T(8,128)S(1)}) all-reduce(f32[17,17]{1,0:T(8,128)S(1)} %get-tuple-element.3281, f32[17,17]{1,0:T(8,128)S(1)} %get-tuple-element.3280), channel_id=1, replica_groups=mesh['gx'=8,'gy'=4] {'gx','gy'}, use_global_device_ids=true, to_apply=%region_8.9 | all-reduce | flops 578 | bytes 4624 | tf_op jit(solution)/shard_map/psum | solution.py:236
  658.0 10.0 conditional.13
  668.6 48.3 %conditional.12 = (f32[8192]{0:T(1024)S(1)}) conditional(s32[]{:T(128)} %convert_element_type.120, () %tuple.70, (f32[17,1]{0,1:T(1,128)S(1)}, f32[8192]{0:T(1024)S(1)}, f32[8192]{0:T(1024)S(1)}, f32[8192]{0:T(1024)S(1)}, f32[17,1]{0,1:T(1,128)S(1)}, /*index=5*/f32[17,1]{0,1:T(1,128)S(1)}, f32[17,17]{1,0:T(8,128)S(1)}, f32[17,1]{0,1:T(1,128)S(1)}, ...), branch_computations={%region_10.11_spmd, %region_11.12_spmd} | conditional | flops 145293392 | bytes 33228644 | solution.py:246
  718.3 15.7 %conditional.15 = (f32[16384]{0:T(1024)S(1)}) conditional(s32[]{:T(128)} %convert_element_type.119, () %tuple.75, (f32[17,1]{0,1:T(1,128)S(1)}, f32[16384]{0:T(1024)}, f32[16384]{0:T(1024)S(1)}, f32[16384]{0:T(1024)S(1)}, f32[17,1]{0,1:T(1,128)S(1)}, /*index=5*/f32[17,1]{0,1:T(1,128)S(1)}, f32[17,17]{1,0:T(8,128)S(1)}, f32[17,1]{0,1:T(1,128)S(1)}, ...), branch_computations={%region_16.17_spmd, %region_17.18_spmd} | conditional | flops 290586688 | bytes 66294256 | solution.py:246
  734.0 81.9 %conditional.14 = (f32[16384]{0:T(1024)S(1)}) conditional(s32[]{:T(128)} %convert_element_type.118, () %tuple.73, (f32[17,1]{0,1:T(1,128)S(1)}, f32[16384]{0:T(1024)}, f32[16384]{0:T(1024)S(1)}, f32[16384]{0:T(1024)S(1)}, f32[17,1]{0,1:T(1,128)S(1)}, /*index=5*/f32[17,1]{0,1:T(1,128)S(1)}, f32[17,17]{1,0:T(8,128)S(1)}, f32[17,1]{0,1:T(1,128)S(1)}, ...), branch_computations={%region_14.15_spmd, %region_15.16_spmd} | conditional | flops 290586688 | bytes 66291856 | solution.py:246
  778.1 6.4 multiply_add_fusion.334
  796.8 6.5 multiply_add_fusion.335
  820.3 23.6 %all_to_all.119 = f32[4,64,256]{2,1,0:T(8,128)S(1)} all-to-all(f32[4,64,256]{2,1,0:T(8,128)S(1)} %pad_maximum_fusion.1), channel_id=1, replica_groups=mesh['gx'=8,'gy'=4] {'gy'}, dimensions={0} | all-to-all | bytes 524288 | tf_op jit(solution)/shard_map/all_to_all | solution.py:170
  854.3 10.7 %all-to-all-done.5 = f32[8,32,320]{2,1,0:T(8,128)S(1)} async-done(((f32[8,32,320]{2,1,0:T(8,128)}), f32[8,32,320]{2,1,0:T(8,128)S(1)}, u32[]{:S(2)}, u32[]{:S(2)}) %all-to-all-start.5) | async-done | bytes 327712 | tf_op jit(solution)/shard_map/all_to_all | solution.py:173
  874.7 8.7 convolution_bitcast_fusion.1
  883.5 6.9 copy.909
  890.4 6.4 reshape.2054
  896.8 51.8 %all_to_all.120 = f32[32,8,2048]{2,0,1:T(8,128)} all-to-all(f32[32,8,2048]{2,0,1:T(8,128)S(1)} %reshape.2054), channel_id=1, replica_groups=mesh['gx'=8,'gy'=4] {'gx'}, dimensions={1} | all-to-all | bytes 4194304 | tf_op jit(solution)/shard_map/all_to_all | solution.py:176
  948.6 6.2 reshape.1207
  954.8 7.0 copy.887
  961.8 7.0 fusion.1204
  971.6 29.2 %all_to_all.121 = f32[64,4,2048]{2,0,1:T(8,128)} all-to-all(f32[64,4,2048]{2,0,1:T(8,128)S(1)} %copy.888), channel_id=1, replica_groups=mesh['gx'=8,'gy'=4] {'gy'}, dimensions={1} | all-to-all | bytes 4194304 | tf_op jit(solution)/shard_map/all_to_all | solution.py:179
  1000.8 5.0 reshape.1208
  1005.8 14.0 %multiply_reduce_fusion.1 = (f32[]{:T(128)}, f32[]{:T(128)}, f32[32,64,256]{2,1,0:T(8,128)}) fusion(f32[32,64,256]{2,1,0:T(8,128)} %param.834, f32[32,64,256]{2,1,0:T(8,128)S(1)} %copy-done.1, s32[256]{0:T(256)S(1)} %copy-done.95, f32[256,32,64]{2,1,0:T(8,128)} %reshape.1208), kind=kOutput, calls=%fused_computation.1798 | convolution fusion | flops 1613299712 | bytes 8389640 | tf_op jit(solution)/shard_map/kab,kz->abz/dot_general | solution.py:159
  1021.1 40.1 %all-reduce = (f32[1]{0:T(128)}, f32[1]{0:T(128)}) all-reduce(f32[1]{0:T(128)} %bitcast.1856, f32[1]{0:T(128)} %bitcast.1855), channel_id=1, replica_groups=mesh['gx'=8,'gy'=4] {'gx','gy'}, use_global_device_ids=true, to_apply=%region_23.24 | all-reduce | flops 2 | bytes 16 | tf_op jit(solution)/shard_map/psum | solution.py:318
  (1332 shorter events, 432.0 us)
Async XLA Ops:
  0.6 275.2 %copy-start.94 = (s32[256]{0:T(256)}, s32[256]{0:T(256)S(1)}, u32[]{:S(2)}) copy-start(s32[256]{0:T(256)S(1)} %iota_add_fusion) | copy-start | bytes 3076
  13.0 29.9 %all-to-all-start = ((f32[4,64,2048]{2,1,0:T(8,128)}), f32[4,64,2048]{2,1,0:T(8,128)S(1)}, u32[]{:S(2)}, u32[]{:S(2)}) async-start(f32[4,64,2048]{2,1,0:T(8,128)} %copy.900), calls=%async_computation | async-start | bytes 4194304 | tf_op jit(solution)/shard_map/all_to_all | solution.py:170
  17.2 120.4 %copy-start.489 = (s32[8,32]{1,0:T(8,128)}, s32[8,32]{1,0:T(8,128)S(1)}, u32[]{:S(2)}) copy-start(s32[8,32]{1,0:T(8,128)S(1)} %add_add_fusion.7) | copy-start | bytes 3076
  55.1 66.2 %all-to-all-start.1 = ((f32[8,32,2048]{2,1,0:T(8,128)}), f32[8,32,2048]{2,1,0:T(8,128)S(1)}, u32[]{:S(2)}, u32[]{:S(2)}) async-start(f32[8,32,2048]{2,1,0:T(8,128)} %convolution_bitcast_fusion), calls=%async_computation.1 | async-start | bytes 4194304 | tf_op jit(solution)/shard_map/all_to_all | solution.py:173
  62.2 63.9 %copy-start.567 = (f32[256]{0:T(256)}, f32[256]{0:T(256)S(1)}, u32[]{:S(2)}) copy-start(f32[256]{0:T(256)S(1)} %multiply_multiply_fusion.64) | copy-start | bytes 3076
  62.3 63.8 %copy-start.467 = (f32[32,64]{1,0:T(8,128)}, f32[32,64]{1,0:T(8,128)S(1)}, u32[]{:S(2)}) copy-start(f32[32,64]{1,0:T(8,128)S(1)} %broadcast_add_fusion) | copy-start | bytes 24580
  160.5 52.0 %all-to-all-start.2 = ((f32[32,8,2048]{2,0,1:T(8,128)}), f32[32,8,2048]{2,0,1:T(8,128)S(1)}, u32[]{:S(2)}, u32[]{:S(2)}) async-start(f32[32,8,2048]{2,0,1:T(8,128)} %reshape.2047), calls=%async_computation.2 | async-start | bytes 4194304 | tf_op jit(solution)/shard_map/all_to_all | solution.py:176
  164.3 60.0 %copy-start.497 = (s32[4,64]{1,0:T(4,128)}, s32[4,64]{1,0:T(4,128)S(1)}, u32[]{:S(2)}) copy-start(s32[4,64]{1,0:T(4,128)S(1)} %add_add_fusion.9) | copy-start | bytes 3076
  235.1 29.2 %all-to-all-start.3 = ((f32[64,4,2048]{2,0,1:T(8,128)}), f32[64,4,2048]{2,0,1:T(8,128)S(1)}, u32[]{:S(2)}, u32[]{:S(2)}) async-start(f32[64,4,2048]{2,0,1:T(8,128)} %copy.873), calls=%async_computation.3 | async-start | bytes 4194304 | tf_op jit(solution)/shard_map/all_to_all | solution.py:179
  240.1 143.1 %copy-start.4 = (f32[8,2,8,128]{3,1,2,0:T(2,128)}, f32[8,2,8,128]{3,1,2,0:T(2,128)S(1)}, u32[]{:S(2)}) copy-start(f32[8,2,8,128]{3,1,2,0:T(2,128)S(1)} %copy.915) | copy-start | bytes 196612
  241.0 88.3 %copy-start.407 = (f32[2048]{0:T(1024)}, f32[2048]{0:T(1024)S(1)}, u32[]{:S(2)}) copy-start(f32[2048]{0:T(1024)S(1)} %get-tuple-element.2775) | copy-start | bytes 24580
  241.0 92.1 %copy-start.405 = (f32[2048]{0:T(1024)}, f32[2048]{0:T(1024)S(1)}, u32[]{:S(2)}) copy-start(f32[2048]{0:T(1024)S(1)} %get-tuple-element.2776) | copy-start | bytes 24580
  241.0 88.2 %copy-start.453 = (f32[2048]{0:T(1024)}, f32[2048]{0:T(1024)S(1)}, u32[]{:S(2)}) copy-start(f32[2048]{0:T(1024)S(1)} %get-tuple-element.3227) | copy-start | bytes 24580
  241.1 88.2 %copy-start.455 = (f32[2048]{0:T(1024)}, f32[2048]{0:T(1024)S(1)}, u32[]{:S(2)}) copy-start(f32[2048]{0:T(1024)S(1)} %get-tuple-element.3225) | copy-start | bytes 24580
  241.1 88.2 %copy-start.457 = (f32[2048]{0:T(1024)}, f32[2048]{0:T(1024)S(1)}, u32[]{:S(2)}) copy-start(f32[2048]{0:T(1024)S(1)} %get-tuple-element.3223) | copy-start | bytes 24580
  241.1 88.2 %copy-start.459 = (f32[2048]{0:T(1024)}, f32[2048]{0:T(1024)S(1)}, u32[]{:S(2)}) copy-start(f32[2048]{0:T(1024)S(1)} %get-tuple-element.3221) | copy-start | bytes 24580
  241.1 88.2 %copy-start.461 = (f32[2048]{0:T(1024)}, f32[2048]{0:T(1024)S(1)}, u32[]{:S(2)}) copy-start(f32[2048]{0:T(1024)S(1)} %get-tuple-element.3219) | copy-start | bytes 24580
  241.1 92.0 %copy-start.443 = (f32[2048]{0:T(1024)}, f32[2048]{0:T(1024)S(1)}, u32[]{:S(2)}) copy-start(f32[2048]{0:T(1024)S(1)} %get-tuple-element.3228) | copy-start | bytes 24580
  241.1 92.0 %copy-start.445 = (f32[2048]{0:T(1024)}, f32[2048]{0:T(1024)S(1)}, u32[]{:S(2)}) copy-start(f32[2048]{0:T(1024)S(1)} %get-tuple-element.3226) | copy-start | bytes 24580
  241.1 92.0 %copy-start.447 = (f32[2048]{0:T(1024)}, f32[2048]{0:T(1024)S(1)}, u32[]{:S(2)}) copy-start(f32[2048]{0:T(1024)S(1)} %get-tuple-element.3224) | copy-start | bytes 24580
  241.1 92.0 %copy-start.449 = (f32[2048]{0:T(1024)}, f32[2048]{0:T(1024)S(1)}, u32[]{:S(2)}) copy-start(f32[2048]{0:T(1024)S(1)} %get-tuple-element.3222) | copy-start | bytes 24580
  241.1 92.0 %copy-start.451 = (f32[2048]{0:T(1024)}, f32[2048]{0:T(1024)S(1)}, u32[]{:S(2)}) copy-start(f32[2048]{0:T(1024)S(1)} %get-tuple-element.3220) | copy-start | bytes 24580
  287.2 226.4 %copy-start = (f32[32,64,256]{2,1,0:T(8,128)}, f32[32,64,256]{2,1,0:T(8,128)S(1)}, u32[]{:S(2)}) copy-start(f32[32,64,256]{2,1,0:T(8,128)S(1)} %fusion.1202) | copy-start | bytes 6291460
  289.3 42.0 %copy-start.463 = (f32[2048]{0:T(1024)}, f32[2048]{0:T(1024)S(1)}, u32[]{:S(2)}) copy-start(f32[2048]{0:T(1024)S(1)} %get-tuple-element.3265) | copy-start | bytes 24580
  289.3 42.0 %copy-start.465 = (f32[2048]{0:T(1024)}, f32[2048]{0:T(1024)S(1)}, u32[]{:S(2)}) copy-start(f32[2048]{0:T(1024)S(1)} %get-tuple-element.3267) | copy-start | bytes 24580
  331.3 38.2 %copy-start.23 = (f32[17,2048]{1,0:T(8,128)}, f32[17,2048]{1,0:T(8,128)S(1)}, u32[]{:S(2)}) copy-start(f32[17,2048]{1,0:T(8,128)S(1)} %get-tuple-element.2765) | copy-start | bytes 417796
  331.3 39.9 %copy-start.27 = (f32[17,2048]{1,0:T(8,128)}, f32[17,2048]{1,0:T(8,128)S(1)}, u32[]{:S(2)}) copy-start(f32[17,2048]{1,0:T(8,128)S(1)} %get-tuple-element.2764) | copy-start | bytes 417796
  383.2 113.2 %copy-start.6 = (f32[4,2,8,128]{3,1,2,0:T(2,128)S(1)}, f32[4,2,8,128]{3,1,2,0:T(2,128)}, u32[]{:S(2)}) copy-start(f32[4,2,8,128]{3,1,2,0:T(2,128)} %copy.917) | copy-start | bytes 98308
  383.3 113.2 %copy-start.78 = (f32[4,2,8,128]{3,1,2,0:T(2,128)S(1)}, f32[4,2,8,128]{3,1,2,0:T(2,128)}, u32[]{:S(2)}) copy-start(f32[4,2,8,128]{3,1,2,0:T(2,128)} %copy.916) | copy-start | bytes 98308
  383.4 54.9 %copy-start.570 = (f32[17]{0:T(128)}, f32[17]{0:T(128)S(1)}, u32[]{:S(2)}) copy-start(f32[17]{0:T(128)S(1)} %multiply_bitcast_fusion.4) | copy-start | bytes 208 | tf_op jit(solution)/shard_map/cond
  383.4 49.8 %copy-start.564 = (f32[17]{0:T(128)}, f32[17]{0:T(128)S(1)}, u32[]{:S(2)}) copy-start(f32[17]{0:T(128)S(1)} %get-tuple-element.2867) | copy-start | bytes 208 | tf_op jit(solution)/shard_map/cond
  385.1 62.1 %copy-start.471 = (f32[16384]{0:T(1024)}, f32[16384]{0:T(1024)S(1)}, u32[]{:S(2)}) copy-start(f32[16384]{0:T(1024)S(1)} %get-tuple-element.2621) | copy-start | bytes 196612 | tf_op jit(solution)/shard_map/cond
  386.2 40.6 %copy-start.86 = (f32[16384]{0:T(1024)}, f32[16384]{0:T(1024)S(1)}, u32[]{:S(2)}) copy-start(f32[16384]{0:T(1024)S(1)} %get-tuple-element.2828) | copy-start | bytes 196612 | tf_op jit(solution)/shard_map/cond
  386.2 47.0 %copy-start.88 = (f32[16384]{0:T(1024)}, f32[16384]{0:T(1024)S(1)}, u32[]{:S(2)}) copy-start(f32[16384]{0:T(1024)S(1)} %get-tuple-element.2830) | copy-start | bytes 196612 | tf_op jit(solution)/shard_map/cond
  386.2 47.0 %copy-start.90 = (f32[16384]{0:T(1024)}, f32[16384]{0:T(1024)S(1)}, u32[]{:S(2)}) copy-start(f32[16384]{0:T(1024)S(1)} %get-tuple-element.2832) | copy-start | bytes 196612 | tf_op jit(solution)/shard_map/cond
  386.2 64.1 %copy-start.477 = (f32[16384]{0:T(1024)}, f32[16384]{0:T(1024)S(1)}, u32[]{:S(2)}) copy-start(f32[16384]{0:T(1024)S(1)} %get-tuple-element.2862) | copy-start | bytes 196612 | tf_op jit(solution)/shard_map/cond
  568.5 57.7 %copy-start.74 = (f32[17,2048]{1,0:T(8,128)S(1)}, f32[17,2048]{1,0:T(8,128)}, u32[]{:S(2)}) copy-start(f32[17,2048]{1,0:T(8,128)} %copy-done.73) | copy-start | bytes 417796
  568.5 57.9 %copy-start.72 = (f32[17,2048]{1,0:T(8,128)S(1)}, f32[17,2048]{1,0:T(8,128)}, u32[]{:S(2)}) copy-start(f32[17,2048]{1,0:T(8,128)} %copy-done.71) | copy-start | bytes 417796
  568.5 58.1 %copy-start.70 = (f32[17,2048]{1,0:T(8,128)S(1)}, f32[17,2048]{1,0:T(8,128)}, u32[]{:S(2)}) copy-start(f32[17,2048]{1,0:T(8,128)} %copy-done.69) | copy-start | bytes 417796
  568.5 58.3 %copy-start.66 = (f32[17,2048]{1,0:T(8,128)S(1)}, f32[17,2048]{1,0:T(8,128)}, u32[]{:S(2)}) copy-start(f32[17,2048]{1,0:T(8,128)} %copy-done.65) | copy-start | bytes 417796
  568.5 58.6 %copy-start.68 = (f32[17,2048]{1,0:T(8,128)S(1)}, f32[17,2048]{1,0:T(8,128)}, u32[]{:S(2)}) copy-start(f32[17,2048]{1,0:T(8,128)} %copy-done.67) | copy-start | bytes 417796
  568.5 58.8 %copy-start.64 = (f32[17,2048]{1,0:T(8,128)S(1)}, f32[17,2048]{1,0:T(8,128)}, u32[]{:S(2)}) copy-start(f32[17,2048]{1,0:T(8,128)} %copy-done.63) | copy-start | bytes 417796
  568.5 59.0 %copy-start.62 = (f32[17,2048]{1,0:T(8,128)S(1)}, f32[17,2048]{1,0:T(8,128)}, u32[]{:S(2)}) copy-start(f32[17,2048]{1,0:T(8,128)} %copy-done.61) | copy-start | bytes 417796
  568.5 59.3 %copy-start.60 = (f32[17,2048]{1,0:T(8,128)S(1)}, f32[17,2048]{1,0:T(8,128)}, u32[]{:S(2)}) copy-start(f32[17,2048]{1,0:T(8,128)} %copy-done.59) | copy-start | bytes 417796
  577.0 51.1 %copy-start.58 = (f32[17,2048]{1,0:T(8,128)S(1)}, f32[17,2048]{1,0:T(8,128)}, u32[]{:S(2)}) copy-start(f32[17,2048]{1,0:T(8,128)} %copy-done.57) | copy-start | bytes 417796
  668.0 49.7 %copy-start.5 = (f32[8,2,8,128]{3,1,2,0:T(2,128)S(1)}, f32[8,2,8,128]{3,1,2,0:T(2,128)}, u32[]{:S(2)}) copy-start(f32[8,2,8,128]{3,1,2,0:T(2,128)} %copy-done.4) | copy-start | bytes 196612
  734.0 82.0 %copy-start.95 = (s32[256]{0:T(256)S(1)}, s32[256]{0:T(256)}, u32[]{:S(2)}) copy-start(s32[256]{0:T(256)} %copy-done.94) | copy-start | bytes 3076
  849.5 15.4 %all-to-all-start.5 = ((f32[8,32,320]{2,1,0:T(8,128)}), f32[8,32,320]{2,1,0:T(8,128)S(1)}, u32[]{:S(2)}, u32[]{:S(2)}) async-start(f32[8,32,320]{2,1,0:T(8,128)} %pad_maximum_fusion), calls=%async_computation.5 | async-start | bytes 786432 | tf_op jit(solution)/shard_map/all_to_all | solution.py:173
  (420 other events, 2775.9 us)
where the time goes:
time: 1080 us; the launch traced here: 1060 us
  matrix products  440 us (41%)
  blocking collectives  185 us (17%)
  waiting for transfers between devices  167 us (15%)
  local copies, waits for them, and re-layouts  122 us (11%)
  loops' own time  62.3 us (6%)
  other arithmetic  59.1 us (5%)
  starting transfers between devices  22 us (2%)
    dot_general x68, matrix products, visitor(): jnp.dot(sine_now, weight, precision=exact_mode)  105 us
    dot_general x68, matrix products, visitor(): jnp.dot(cosine_now, weight, precision=exact_mode)  102 us
    dot_general x68, matrix products, visitor(): jnp.dot(weight_cosine[degree], cosine_now, precision=exact_mode)  71.4 us
    all_to_all x2, waiting for transfers between devices, swap_two(): lax.all_to_all(operand, 'gx', split_axis=0, concat_axis=1, tiled=True)  69.7 us
    dot_general x68, matrix products, visitor(): return accum + jnp.dot(weight_sine[degree], sine_now, precision=exact_mode)  65.3 us
    all_to_all x1, blocking collectives, back_two(): lax.all_to_all(operand, 'gx', split_axis=1, concat_axis=0, tiled=True)  51.8 us
    all_to_all x1, waiting for transfers between devices, back_two(): lax.all_to_all(operand, 'gx', split_axis=1, concat_axis=0, tiled=True)  48.2 us
    psum x1, blocking collectives, shards(): sum_cosine, sum_sine = lax.psum((mom_cosine, mom_sine), ('gx', 'gy'))  40.4 us
  transfers between devices with their start and end apart: 5, of which 5 were waited for; matrix products, arithmetic and copies ran while one was open for 0% of the time, Pallas kernels for 0%

commit v1 on v0

--- a/solution.py
+++ b/solution.py
@@ -1,3 +1,4 @@
+import functools
 import math
 import jax
 import jax.numpy as jnp
@@ -9,6 +10,16 @@
 exact_mode = lax.Precision.HIGHEST
 outer_ratio = 1.1
 radius_scale = math.sqrt(3.0) / 2.0
+
+
+def bring_the_counts(xx, axis_name):
+    clean = jnp.split(xx, jax.lax.axis_size(axis_name), axis=1)
+    z2 = jnp.stack(clean, axis=0)
+    arr_now = jax.lax.all_to_all(z2, axis_name=axis_name, split_axis=0, concat_axis=0)
+    return jnp.concatenate(arr_now, axis=0)
+
+
+assign_the_quotas = functools.partial(bring_the_counts, axis_name="gy")
 
 
 def sine_table(length):
@@ -176,7 +187,7 @@
         return lax.all_to_all(operand, "gx", split_axis=1, concat_axis=0, tiled=True)
 
     def back_one(operand):
-        return lax.all_to_all(operand, "gy", split_axis=1, concat_axis=0, tiled=True)
+        return assign_the_quotas(operand)
 
     groups_one = lax.axis_size("gy")
     groups_two = lax.axis_size("gx")

time: 1080 us -> 1070 us (level)
  waiting for transfers between devices: 167 us -> 155 us
    reshape x2 -> x0, local copies, waits for them, and re-layouts: 16.5 us -> none  [inverse(): volume = volume.reshape(length, cells_a, cells_b)]
    unnamed x498 -> x518, local copies, waits for them, and re-layouts: 6.51 us -> 17.8 us
    all_to_all x2, waiting for transfers between devices: 69.7 us -> 58.5 us  [swap_two(): lax.all_to_all(operand, 'gx', split_axis=0, concat_axis=1, tiled=True)]
where the time goes in v1:
time: 1070 us; the launch traced here: 1060 us
  matrix products  435 us (41%)
  blocking collectives  193 us (18%)
  waiting for transfers between devices  155 us (14%)
  local copies, waits for them, and re-layouts  121 us (11%)
  loops' own time  62.3 us (6%)
  other arithmetic  60.7 us (6%)
  starting transfers between devices  22.4 us (2%)
    dot_general x68, matrix products, visitor(): jnp.dot(sine_now, weight, precision=exact_mode)  105 us
    dot_general x68, matrix products, visitor(): jnp.dot(cosine_now, weight, precision=exact_mode)  102 us
    dot_general x68, matrix products, visitor(): jnp.dot(weight_cosine[degree], cosine_now, precision=exact_mode)  71.4 us
    dot_general x68, matrix products, visitor(): return accum + jnp.dot(weight_sine[degree], sine_now, precision=exact_mode)  65.3 us
    all_to_all x2, waiting for transfers between devices, swap_two(): lax.all_to_all(operand, 'gx', split_axis=0, concat_axis=1, tiled=True)  58.5 us
    all_to_all x1, blocking collectives, back_two(): lax.all_to_all(operand, 'gx', split_axis=1, concat_axis=0, tiled=True)  51.5 us
    all_to_all x1, waiting for transfers between devices, back_two(): lax.all_to_all(operand, 'gx', split_axis=1, concat_axis=0, tiled=True)  47.9 us
    psum x1, blocking collectives, shards(): sum_cosine, sum_sine = lax.psum((mom_cosine, mom_sine), ('gx', 'gy'))  47.8 us
  transfers between devices with their start and end apart: 5, of which 5 were waited for; matrix products, arithmetic and copies ran while one was open for 0% of the time, Pallas kernels for 0%

profile of v1, /device:TPU:0, one launch (start us, length us, event | category | flops | bytes accessed | tf_op | source)
XLA Modules:
  0.0 1055.8 jit_solution(10771726672896726292)
XLA Ops:
  0.6 4.5 fusion.1266
  8.2 4.7 copy.918
  13.0 4.2 all-to-all-start
  17.3 25.6 %all-to-all-done = f32[4,64,2048]{2,1,0:T(8,128)S(1)} async-done(((f32[4,64,2048]{2,1,0:T(8,128)}), f32[4,64,2048]{2,1,0:T(8,128)S(1)}, u32[]{:S(2)}, u32[]{:S(2)}) %all-to-all-start) | async-done | bytes 2097184 | tf_op jit(solution)/shard_map/all_to_all | solution.py:181
  45.9 9.2 convolution_bitcast_fusion
  55.1 6.9 all-to-all-start.1
  62.2 48.0 %all-to-all-done.1 = f32[8,32,2048]{2,1,0:T(8,128)S(1)} async-done(((f32[8,32,2048]{2,1,0:T(8,128)}), f32[8,32,2048]{2,1,0:T(8,128)S(1)}, u32[]{:S(2)}, u32[]{:S(2)}) %all-to-all-start.1) | async-done | bytes 2097184 | tf_op jit(solution)/shard_map/all_to_all | solution.py:184
  110.3 4.8 reshape.2034
  115.0 11.5 %bitcast_divide_fusion = f32[32,64,256]{2,1,0:T(8,128)S(1)} fusion(f32[32,8,64,32]{3,2,0,1:T(8,128)} %reshape.2034, f32[256]{0:T(256)S(1)} %multiply_multiply_fusion.64, f32[32,64]{1,0:T(8,128)S(1)} %broadcast_add_fusion, s32[256]{0:T(256)S(1)} %iota_add_fusion, s32[8,32]{1,0:T(8,128)S(1)} %add_add_fusion.7), kind=kOutput, calls=%fused_computation.1785 | convolution fusion | flops 1612775424 | bytes 4205568 | tf_op jit(solution)/shard_map/kqzc,qcj->kzj/dot_general | solution.py:155
  127.9 7.0 convolution_bitcast_fusion.2
  135.0 6.9 copy.923
  141.9 7.5 reshape.2035
  153.6 47.9 %all-to-all-done.2 = f32[32,8,2048]{2,0,1:T(8,128)S(1)} async-done(((f32[32,8,2048]{2,0,1:T(8,128)}), f32[32,8,2048]{2,0,1:T(8,128)S(1)}, u32[]{:S(2)}, u32[]{:S(2)}) %all-to-all-start.2) | async-done | bytes 2097184 | tf_op jit(solution)/shard_map/all_to_all | solution.py:187
  201.5 4.8 reshape.1185
  206.3 7.0 copy.884
  213.3 4.6 fusion.1211
  232.3 23.1 %all-to-all-done.3 = f32[4,64,2048]{2,1,0:T(8,128)S(1)} async-done(((f32[4,64,2048]{2,1,0:T(8,128)}), f32[4,64,2048]{2,1,0:T(8,128)S(1)}, u32[]{:S(2)}, u32[]{:S(2)}) %all-to-all-start.3) | async-done | bytes 2097184 | tf_op jit(solution)/shard_map/all_to_all | solution.py:18
  258.7 11.3 %fusion.1202 = f32[32,64,256]{2,1,0:T(8,128)S(1)} fusion(f32[256,32,64]{2,1,0:T(8,128)} %reshape_reshape.6, s32[256]{0:T(256)S(1)} %iota_add_fusion), kind=kOutput, calls=%fused_computation.1780 | convolution fusion | flops 1611202560 | bytes 4195328 | tf_op jit(solution)/shard_map/kab,kz->abz/dot_general | solution.py:170
  356.1 10.0 conditional.9
  366.1 113.1 %conditional.8 = (f32[17,17]{1,0:T(8,128)S(1)}, f32[17,17]{1,0:T(8,128)S(1)}) conditional(s32[]{:T(128)} %convert_element_type.118, () %tuple.64, (f32[17,1]{0,1:T(1,128)S(1)}, f32[16384]{0:T(1024)}, f32[16384]{0:T(1024)S(1)}, f32[16384]{0:T(1024)S(1)}, f32[17,1]{0,1:T(1,128)S(1)}, /*index=5*/f32[17,1]{0,1:T(1,128)S(1)}, ...), branch_computations={%region_0.1_spmd, %region_1.2_spmd} | conditional | flops 290816064 | bytes 57925084 | solution.py:241
  374.4 4.6 fusion.115
  379.0 4.5 fusion.114
  383.5 4.3 fusion.113
  387.7 4.1 fusion.112
  423.6 6.4 multiply_add_fusion.2
  454.9 7.8 multiply_add_fusion.17
  479.9 16.6 %conditional.11 = (f32[17,17]{1,0:T(8,128)S(1)}, f32[17,17]{1,0:T(8,128)S(1)}) conditional(s32[]{:T(128)} %convert_element_type.121, () %tuple.69, (f32[17,1]{0,1:T(1,128)S(1)}, f32[8192]{0:T(1024)S(1)}, f32[8192]{0:T(1024)S(1)}, f32[8192]{0:T(1024)S(1)}, f32[17,1]{0,1:T(1,128)S(1)}, /*index=5*/f32[17,1]{0,1:T(1,128)S(1)}, ...), branch_computations={%region_6.7_spmd, %region_7.8_spmd} | conditional | flops 145408080 | bytes 28004404 | solution.py:241
  497.0 54.3 %conditional.10 = (f32[17,17]{1,0:T(8,128)}, f32[17,17]{1,0:T(8,128)}) conditional(s32[]{:T(128)} %convert_element_type.120, () %tuple.67, (f32[17,1]{0,1:T(1,128)S(1)}, f32[8192]{0:T(1024)S(1)}, f32[8192]{0:T(1024)S(1)}, f32[8192]{0:T(1024)S(1)}, f32[17,1]{0,1:T(1,128)S(1)}, /*index=5*/f32[17,1]{0,1:T(1,128)S(1)}, f32[32,64,256]{2,1,0:T(8,128)S(1)}, ...), branch_computations={%region_4.5_spmd, %region_5.6_spmd} | conditional | flops 145408080 | bytes 27208952 | solution.py:241
  560.6 47.8 %all-reduce.1 = (f32[17,17]{1,0:T(8,128)S(1)}, f32[17,17]{1,0:T(8,128)S(1)}) all-reduce(f32[17,17]{1,0:T(8,128)S(1)} %get-tuple-element.3289, f32[17,17]{1,0:T(8,128)S(1)} %get-tuple-element.3288), channel_id=1, replica_groups=mesh['gx'=8,'gy'=4] {'gx','gy'}, use_global_device_ids=true, to_apply=%region_8.9 | all-reduce | flops 578 | bytes 4624 | tf_op jit(solution)/shard_map/psum | solution.py:247
  648.2 10.0 conditional.13
  658.8 48.3 %conditional.12 = (f32[8192]{0:T(1024)S(1)}) conditional(s32[]{:T(128)} %convert_element_type.120, () %tuple.70, (f32[17,1]{0,1:T(1,128)S(1)}, f32[8192]{0:T(1024)S(1)}, f32[8192]{0:T(1024)S(1)}, f32[8192]{0:T(1024)S(1)}, f32[17,1]{0,1:T(1,128)S(1)}, /*index=5*/f32[17,1]{0,1:T(1,128)S(1)}, f32[17,17]{1,0:T(8,128)S(1)}, f32[17,1]{0,1:T(1,128)S(1)}, ...), branch_computations={%region_10.11_spmd, %region_11.12_spmd} | conditional | flops 145293392 | bytes 33228644 | solution.py:257
  708.5 15.7 %conditional.15 = (f32[16384]{0:T(1024)S(1)}) conditional(s32[]{:T(128)} %convert_element_type.119, () %tuple.75, (f32[17,1]{0,1:T(1,128)S(1)}, f32[16384]{0:T(1024)}, f32[16384]{0:T(1024)S(1)}, f32[16384]{0:T(1024)S(1)}, f32[17,1]{0,1:T(1,128)S(1)}, /*index=5*/f32[17,1]{0,1:T(1,128)S(1)}, f32[17,17]{1,0:T(8,128)S(1)}, f32[17,1]{0,1:T(1,128)S(1)}, ...), branch_computations={%region_16.17_spmd, %region_17.18_spmd} | conditional | flops 290586688 | bytes 66294256 | solution.py:257
  724.3 81.9 %conditional.14 = (f32[16384]{0:T(1024)S(1)}) conditional(s32[]{:T(128)} %convert_element_type.118, () %tuple.73, (f32[17,1]{0,1:T(1,128)S(1)}, f32[16384]{0:T(1024)}, f32[16384]{0:T(1024)S(1)}, f32[16384]{0:T(1024)S(1)}, f32[17,1]{0,1:T(1,128)S(1)}, /*index=5*/f32[17,1]{0,1:T(1,128)S(1)}, f32[17,17]{1,0:T(8,128)S(1)}, f32[17,1]{0,1:T(1,128)S(1)}, ...), branch_computations={%region_14.15_spmd, %region_15.16_spmd} | conditional | flops 290586688 | bytes 66291856 | solution.py:257
  768.4 6.4 multiply_add_fusion.334
  787.0 6.5 multiply_add_fusion.335
  810.5 24.3 %all_to_all.97 = f32[4,64,256]{2,1,0:T(8,128)S(1)} all-to-all(f32[4,64,256]{2,1,0:T(8,128)S(1)} %pad_maximum_fusion.3), channel_id=1, replica_groups=mesh['gx'=8,'gy'=4] {'gy'}, dimensions={0} | all-to-all | bytes 524288 | tf_op jit(solution)/shard_map/all_to_all | solution.py:181
  845.2 10.5 all-to-all-done.5
  865.5 8.7 convolution_bitcast_fusion.1
  874.2 6.9 copy.927
  881.1 6.4 reshape.2042
  887.6 51.5 %all_to_all.98 = f32[32,8,2048]{2,0,1:T(8,128)} all-to-all(f32[32,8,2048]{2,0,1:T(8,128)S(1)} %reshape.2042), channel_id=1, replica_groups=mesh['gx'=8,'gy'=4] {'gx'}, dimensions={1} | all-to-all | bytes 4194304 | tf_op jit(solution)/shard_map/all_to_all | solution.py:187
  939.1 6.2 reshape.1195
  945.3 7.0 copy.902
  952.3 4.5 fusion.1204
  964.1 29.2 %all_to_all.99 = f32[4,64,2048]{2,1,0:T(8,128)} all-to-all(f32[4,64,2048]{2,1,0:T(8,128)S(1)} %pad_maximum_fusion.1), channel_id=1, replica_groups=mesh['gx'=8,'gy'=4] {'gy'}, dimensions={0} | all-to-all | bytes 4194304 | tf_op jit(solution)/shard_map/all_to_all | solution.py:18
  993.2 5.0 reshape_reshape.7
  998.3 14.1 %multiply_reduce_fusion.1 = (f32[]{:T(128)}, f32[]{:T(128)}, f32[32,64,256]{2,1,0:T(8,128)}) fusion(f32[32,64,256]{2,1,0:T(8,128)} %param.834, f32[32,64,256]{2,1,0:T(8,128)S(1)} %copy-done.1, s32[256]{0:T(256)S(1)} %copy-done.101, f32[256,32,64]{2,1,0:T(8,128)} %reshape_reshape.7), kind=kOutput, calls=%fused_computation.1800 | convolution fusion | flops 1613299712 | bytes 8389640 | tf_op jit(solution)/shard_map/kab,kz->abz/dot_general | solution.py:170
  1013.6 39.9 %all-reduce = (f32[1]{0:T(128)}, f32[1]{0:T(128)}) all-reduce(f32[1]{0:T(128)} %bitcast.1864, f32[1]{0:T(128)} %bitcast.1863), channel_id=1, replica_groups=mesh['gx'=8,'gy'=4] {'gx','gy'}, use_global_device_ids=true, to_apply=%region_23.24 | all-reduce | flops 2 | bytes 16 | tf_op jit(solution)/shard_map/psum | solution.py:329
  (1354 shorter events, 440.3 us)
Async XLA Ops:
  0.6 258.0 %copy-start.100 = (s32[256]{0:T(256)}, s32[256]{0:T(256)S(1)}, u32[]{:S(2)}) copy-start(s32[256]{0:T(256)S(1)} %iota_add_fusion) | copy-start | bytes 3076
  13.0 29.9 %all-to-all-start = ((f32[4,64,2048]{2,1,0:T(8,128)}), f32[4,64,2048]{2,1,0:T(8,128)S(1)}, u32[]{:S(2)}, u32[]{:S(2)}) async-start(f32[4,64,2048]{2,1,0:T(8,128)} %copy.918), calls=%async_computation | async-start | bytes 4194304 | tf_op jit(solution)/shard_map/all_to_all | solution.py:181
  17.3 109.3 %copy-start.495 = (s32[8,32]{1,0:T(8,128)}, s32[8,32]{1,0:T(8,128)S(1)}, u32[]{:S(2)}) copy-start(s32[8,32]{1,0:T(8,128)S(1)} %add_add_fusion.7) | copy-start | bytes 3076
  55.1 55.2 %all-to-all-start.1 = ((f32[8,32,2048]{2,1,0:T(8,128)}), f32[8,32,2048]{2,1,0:T(8,128)S(1)}, u32[]{:S(2)}, u32[]{:S(2)}) async-start(f32[8,32,2048]{2,1,0:T(8,128)} %convolution_bitcast_fusion), calls=%async_computation.1 | async-start | bytes 4194304 | tf_op jit(solution)/shard_map/all_to_all | solution.py:184
  62.2 52.9 %copy-start.573 = (f32[256]{0:T(256)}, f32[256]{0:T(256)S(1)}, u32[]{:S(2)}) copy-start(f32[256]{0:T(256)S(1)} %multiply_multiply_fusion.64) | copy-start | bytes 3076
  62.2 52.8 %copy-start.473 = (f32[32,64]{1,0:T(8,128)}, f32[32,64]{1,0:T(8,128)S(1)}, u32[]{:S(2)}) copy-start(f32[32,64]{1,0:T(8,128)S(1)} %broadcast_add_fusion) | copy-start | bytes 24580
  149.4 52.1 %all-to-all-start.2 = ((f32[32,8,2048]{2,0,1:T(8,128)}), f32[32,8,2048]{2,0,1:T(8,128)S(1)}, u32[]{:S(2)}, u32[]{:S(2)}) async-start(f32[32,8,2048]{2,0,1:T(8,128)} %reshape.2035), calls=%async_computation.2 | async-start | bytes 4194304 | tf_op jit(solution)/shard_map/all_to_all | solution.py:187
  153.6 59.7 %copy-start.503 = (s32[4,64]{1,0:T(4,128)}, s32[4,64]{1,0:T(4,128)S(1)}, u32[]{:S(2)}) copy-start(s32[4,64]{1,0:T(4,128)S(1)} %add_add_fusion.9) | copy-start | bytes 3076
  226.2 29.2 %all-to-all-start.3 = ((f32[4,64,2048]{2,1,0:T(8,128)}), f32[4,64,2048]{2,1,0:T(8,128)S(1)}, u32[]{:S(2)}, u32[]{:S(2)}) async-start(f32[4,64,2048]{2,1,0:T(8,128)} %pad_maximum_fusion), calls=%async_computation.3 | async-start | bytes 4194304 | tf_op jit(solution)/shard_map/all_to_all | solution.py:18
  231.3 134.8 %copy-start.4 = (f32[8,2,8,128]{3,1,2,0:T(2,128)}, f32[8,2,8,128]{3,1,2,0:T(2,128)S(1)}, u32[]{:S(2)}) copy-start(f32[8,2,8,128]{3,1,2,0:T(2,128)S(1)} %copy.941) | copy-start | bytes 196612
  232.2 80.0 %copy-start.413 = (f32[2048]{0:T(1024)}, f32[2048]{0:T(1024)S(1)}, u32[]{:S(2)}) copy-start(f32[2048]{0:T(1024)S(1)} %get-tuple-element.2775) | copy-start | bytes 24580
  232.2 83.9 %copy-start.411 = (f32[2048]{0:T(1024)}, f32[2048]{0:T(1024)S(1)}, u32[]{:S(2)}) copy-start(f32[2048]{0:T(1024)S(1)} %get-tuple-element.2776) | copy-start | bytes 24580
  232.2 79.9 %copy-start.459 = (f32[2048]{0:T(1024)}, f32[2048]{0:T(1024)S(1)}, u32[]{:S(2)}) copy-start(f32[2048]{0:T(1024)S(1)} %get-tuple-element.3235) | copy-start | bytes 24580
  232.3 79.9 %copy-start.461 = (f32[2048]{0:T(1024)}, f32[2048]{0:T(1024)S(1)}, u32[]{:S(2)}) copy-start(f32[2048]{0:T(1024)S(1)} %get-tuple-element.3233) | copy-start | bytes 24580
  232.3 79.9 %copy-start.463 = (f32[2048]{0:T(1024)}, f32[2048]{0:T(1024)S(1)}, u32[]{:S(2)}) copy-start(f32[2048]{0:T(1024)S(1)} %get-tuple-element.3231) | copy-start | bytes 24580
  232.3 79.9 %copy-start.465 = (f32[2048]{0:T(1024)}, f32[2048]{0:T(1024)S(1)}, u32[]{:S(2)}) copy-start(f32[2048]{0:T(1024)S(1)} %get-tuple-element.3229) | copy-start | bytes 24580
  232.3 79.9 %copy-start.467 = (f32[2048]{0:T(1024)}, f32[2048]{0:T(1024)S(1)}, u32[]{:S(2)}) copy-start(f32[2048]{0:T(1024)S(1)} %get-tuple-element.3227) | copy-start | bytes 24580
  232.3 83.7 %copy-start.449 = (f32[2048]{0:T(1024)}, f32[2048]{0:T(1024)S(1)}, u32[]{:S(2)}) copy-start(f32[2048]{0:T(1024)S(1)} %get-tuple-element.3236) | copy-start | bytes 24580
  232.3 83.7 %copy-start.451 = (f32[2048]{0:T(1024)}, f32[2048]{0:T(1024)S(1)}, u32[]{:S(2)}) copy-start(f32[2048]{0:T(1024)S(1)} %get-tuple-element.3234) | copy-start | bytes 24580
  232.3 83.7 %copy-start.453 = (f32[2048]{0:T(1024)}, f32[2048]{0:T(1024)S(1)}, u32[]{:S(2)}) copy-start(f32[2048]{0:T(1024)S(1)} %get-tuple-element.3232) | copy-start | bytes 24580
  232.3 83.7 %copy-start.455 = (f32[2048]{0:T(1024)}, f32[2048]{0:T(1024)S(1)}, u32[]{:S(2)}) copy-start(f32[2048]{0:T(1024)S(1)} %get-tuple-element.3230) | copy-start | bytes 24580
  232.3 83.7 %copy-start.457 = (f32[2048]{0:T(1024)}, f32[2048]{0:T(1024)S(1)}, u32[]{:S(2)}) copy-start(f32[2048]{0:T(1024)S(1)} %get-tuple-element.3228) | copy-start | bytes 24580
  270.0 226.4 %copy-start = (f32[32,64,256]{2,1,0:T(8,128)}, f32[32,64,256]{2,1,0:T(8,128)S(1)}, u32[]{:S(2)}) copy-start(f32[32,64,256]{2,1,0:T(8,128)S(1)} %fusion.1202) | copy-start | bytes 6291460
  272.1 42.1 %copy-start.469 = (f32[2048]{0:T(1024)}, f32[2048]{0:T(1024)S(1)}, u32[]{:S(2)}) copy-start(f32[2048]{0:T(1024)S(1)} %get-tuple-element.3273) | copy-start | bytes 24580
  272.1 42.1 %copy-start.471 = (f32[2048]{0:T(1024)}, f32[2048]{0:T(1024)S(1)}, u32[]{:S(2)}) copy-start(f32[2048]{0:T(1024)S(1)} %get-tuple-element.3275) | copy-start | bytes 24580
  314.2 38.1 %copy-start.29 = (f32[17,2048]{1,0:T(8,128)}, f32[17,2048]{1,0:T(8,128)S(1)}, u32[]{:S(2)}) copy-start(f32[17,2048]{1,0:T(8,128)S(1)} %get-tuple-element.2765) | copy-start | bytes 417796
  314.2 39.8 %copy-start.33 = (f32[17,2048]{1,0:T(8,128)}, f32[17,2048]{1,0:T(8,128)S(1)}, u32[]{:S(2)}) copy-start(f32[17,2048]{1,0:T(8,128)S(1)} %get-tuple-element.2764) | copy-start | bytes 417796
  366.1 113.2 %copy-start.6 = (f32[4,2,8,128]{3,1,2,0:T(2,128)S(1)}, f32[4,2,8,128]{3,1,2,0:T(2,128)}, u32[]{:S(2)}) copy-start(f32[4,2,8,128]{3,1,2,0:T(2,128)} %copy.943) | copy-start | bytes 98308
  366.1 113.2 %copy-start.84 = (f32[4,2,8,128]{3,1,2,0:T(2,128)S(1)}, f32[4,2,8,128]{3,1,2,0:T(2,128)}, u32[]{:S(2)}) copy-start(f32[4,2,8,128]{3,1,2,0:T(2,128)} %copy.942) | copy-start | bytes 98308
  366.2 55.0 %copy-start.576 = (f32[17]{0:T(128)}, f32[17]{0:T(128)S(1)}, u32[]{:S(2)}) copy-start(f32[17]{0:T(128)S(1)} %multiply_bitcast_fusion.4) | copy-start | bytes 208 | tf_op jit(solution)/shard_map/cond
  366.2 49.7 %copy-start.570 = (f32[17]{0:T(128)}, f32[17]{0:T(128)S(1)}, u32[]{:S(2)}) copy-start(f32[17]{0:T(128)S(1)} %get-tuple-element.2867) | copy-start | bytes 208 | tf_op jit(solution)/shard_map/cond
  368.0 62.1 %copy-start.477 = (f32[16384]{0:T(1024)}, f32[16384]{0:T(1024)S(1)}, u32[]{:S(2)}) copy-start(f32[16384]{0:T(1024)S(1)} %get-tuple-element.2621) | copy-start | bytes 196612 | tf_op jit(solution)/shard_map/cond
  369.0 40.6 %copy-start.92 = (f32[16384]{0:T(1024)}, f32[16384]{0:T(1024)S(1)}, u32[]{:S(2)}) copy-start(f32[16384]{0:T(1024)S(1)} %get-tuple-element.2828) | copy-start | bytes 196612 | tf_op jit(solution)/shard_map/cond
  369.0 46.9 %copy-start.94 = (f32[16384]{0:T(1024)}, f32[16384]{0:T(1024)S(1)}, u32[]{:S(2)}) copy-start(f32[16384]{0:T(1024)S(1)} %get-tuple-element.2830) | copy-start | bytes 196612 | tf_op jit(solution)/shard_map/cond
  369.0 46.9 %copy-start.96 = (f32[16384]{0:T(1024)}, f32[16384]{0:T(1024)S(1)}, u32[]{:S(2)}) copy-start(f32[16384]{0:T(1024)S(1)} %get-tuple-element.2832) | copy-start | bytes 196612 | tf_op jit(solution)/shard_map/cond
  369.1 64.2 %copy-start.483 = (f32[16384]{0:T(1024)}, f32[16384]{0:T(1024)S(1)}, u32[]{:S(2)}) copy-start(f32[16384]{0:T(1024)S(1)} %get-tuple-element.2862) | copy-start | bytes 196612 | tf_op jit(solution)/shard_map/cond
  551.3 65.0 %copy-start.80 = (f32[17,2048]{1,0:T(8,128)S(1)}, f32[17,2048]{1,0:T(8,128)}, u32[]{:S(2)}) copy-start(f32[17,2048]{1,0:T(8,128)} %copy-done.79) | copy-start | bytes 417796
  551.3 65.2 %copy-start.78 = (f32[17,2048]{1,0:T(8,128)S(1)}, f32[17,2048]{1,0:T(8,128)}, u32[]{:S(2)}) copy-start(f32[17,2048]{1,0:T(8,128)} %copy-done.77) | copy-start | bytes 417796
  551.4 65.5 %copy-start.76 = (f32[17,2048]{1,0:T(8,128)S(1)}, f32[17,2048]{1,0:T(8,128)}, u32[]{:S(2)}) copy-start(f32[17,2048]{1,0:T(8,128)} %copy-done.75) | copy-start | bytes 417796
  551.4 65.7 %copy-start.72 = (f32[17,2048]{1,0:T(8,128)S(1)}, f32[17,2048]{1,0:T(8,128)}, u32[]{:S(2)}) copy-start(f32[17,2048]{1,0:T(8,128)} %copy-done.71) | copy-start | bytes 417796
  551.4 65.9 %copy-start.74 = (f32[17,2048]{1,0:T(8,128)S(1)}, f32[17,2048]{1,0:T(8,128)}, u32[]{:S(2)}) copy-start(f32[17,2048]{1,0:T(8,128)} %copy-done.73) | copy-start | bytes 417796
  551.4 66.2 %copy-start.70 = (f32[17,2048]{1,0:T(8,128)S(1)}, f32[17,2048]{1,0:T(8,128)}, u32[]{:S(2)}) copy-start(f32[17,2048]{1,0:T(8,128)} %copy-done.69) | copy-start | bytes 417796
  551.4 66.4 %copy-start.68 = (f32[17,2048]{1,0:T(8,128)S(1)}, f32[17,2048]{1,0:T(8,128)}, u32[]{:S(2)}) copy-start(f32[17,2048]{1,0:T(8,128)} %copy-done.67) | copy-start | bytes 417796
  551.4 66.6 %copy-start.66 = (f32[17,2048]{1,0:T(8,128)S(1)}, f32[17,2048]{1,0:T(8,128)}, u32[]{:S(2)}) copy-start(f32[17,2048]{1,0:T(8,128)} %copy-done.65) | copy-start | bytes 417796
  559.8 58.5 %copy-start.64 = (f32[17,2048]{1,0:T(8,128)S(1)}, f32[17,2048]{1,0:T(8,128)}, u32[]{:S(2)}) copy-start(f32[17,2048]{1,0:T(8,128)} %copy-done.63) | copy-start | bytes 417796
  658.2 49.7 %copy-start.5 = (f32[8,2,8,128]{3,1,2,0:T(2,128)S(1)}, f32[8,2,8,128]{3,1,2,0:T(2,128)}, u32[]{:S(2)}) copy-start(f32[8,2,8,128]{3,1,2,0:T(2,128)} %copy-done.4) | copy-start | bytes 196612
  724.2 82.0 %copy-start.101 = (s32[256]{0:T(256)S(1)}, s32[256]{0:T(256)}, u32[]{:S(2)}) copy-start(s32[256]{0:T(256)} %copy-done.100) | copy-start | bytes 3076
  840.5 15.2 %all-to-all-start.5 = ((f32[8,32,320]{2,1,0:T(8,128)}), f32[8,32,320]{2,1,0:T(8,128)S(1)}, u32[]{:S(2)}, u32[]{:S(2)}) async-start(f32[8,32,320]{2,1,0:T(8,128)} %pad_maximum_fusion.2), calls=%async_computation.5 | async-start | bytes 786432 | tf_op jit(solution)/shard_map/all_to_all | solution.py:184
  (426 other events, 2787.4 us)
